TPU v7x, 128 devices: a whole 4x4x4 slice. The times are simulated.
128 devices in a mesh: grp: 8 (over z, y_lo), slab: 16 (over y_hi, x, core).
Axes of the slice: x: 4, y: 4 (y_hi: 2, y_lo: 2; y = y_hi * 2 + y_lo), z: 4, core: 2. Of those that a mesh axis runs over, the one named last changes fastest.
Arguments:
- orbitals: float32 [16, 96, 9216], P('grp', 'slab'), may hold values from -6 to 6
- occupation: int32 [16], P('grp'), may hold values from 1 to 4
- kernel_hat: float32 [192, 36864], P('slab'), may hold values from 0.02 to 1200, as said below
- pair_mask: int32 [1], replicated, may hold values from 1 to 7
Outputs:
- exchange_terms: float32 [16, 96, 9216], P('grp', 'slab')
Inputs may be any that keep to these rules, and one draw needn't show every extreme that they name: In this round group g is paired with group g XOR pair_mask. kernel_hat is positive, and unchanged when each frequency index k is replaced by (192 - k) mod 192 in all three dimensions at once.
All inputs are finite; a program needn't handle non-finite values.
Results may differ from a plain program's by a relative error of at most 0.0001.
Values sent between devices are 32-bit elements; how exact they have to be, the bound alone decides.
No kernel may reach another device: no remote copies, remote signals or barrier semaphores. Data moves between devices by JAX's collectives and lax.ppermute only.
A program may use at most 64 MiB of HBM per device.

v0:
```python
import math

import jax
import jax.numpy as jnp
from jax import lax
from jax.sharding import PartitionSpec as P

G = 96


def swapped(value, axis, apart):
    mask = 2**apart
    pairs = [(source, source ^ mask) for source in range(lax.axis_size(axis))]
    return lax.ppermute(value, axis, pairs)


def dft_tables(size_in, size_out, period):
    row_index = lax.broadcasted_iota(jnp.int32, (size_in, size_out), 0)
    col_index = lax.broadcasted_iota(jnp.int32, (size_in, size_out), 1)
    phase_angle = (row_index * col_index % period).astype(jnp.float32) * (2.0 * math.pi / period)
    return (jnp.cos(phase_angle), jnp.sin(phase_angle))


def contract(form, left, right):
    return jnp.einsum(
        form, left, right, precision=lax.Precision.HIGHEST, preferred_element_type=jnp.float32
    )


def local(orbitals, occupation, kernel_hat, pair_mask):
    orbit_count = orbitals.shape[0]
    half_count = orbit_count // 2
    plane_count = orbitals.shape[1]
    grid_len = G
    padded_len = 2 * G
    kernel_cube = kernel_hat.reshape(kernel_hat.shape[0], padded_len, padded_len)
    cos_fwd, sin_fwd = dft_tables(grid_len, padded_len, padded_len)
    cos_inv, sin_inv = dft_tables(padded_len, grid_len, padded_len)
    cos_inv = cos_inv / padded_len
    sin_inv = sin_inv / padded_len
    forward_pair = jnp.stack([jnp.stack([cos_fwd, -sin_fwd]), jnp.stack([sin_fwd, cos_fwd])])
    inverse_pair = jnp.stack([jnp.stack([cos_inv, sin_inv]), jnp.stack([-sin_inv, cos_inv])])

    def line_work(pencils):
        y_spectra = contract("nckxy,cdyl->ndkxl", pencils, forward_pair)
        spectra = contract("nckxl,cdxm->ndklm", y_spectra, forward_pair)
        spectra = spectra * kernel_cube[None, None]
        x_back = contract("ncklm,cdmx->ndklx", spectra, inverse_pair)
        return contract("ncklx,cdly->ndkxy", x_back, inverse_pair)

    def packed_potential(density_pair):
        spread = contract("ncxyz,cdzk->ndkxy", density_pair, forward_pair)
        planes = lax.all_to_all(
            line_work(lax.all_to_all(spread, "slab", split_axis=2, concat_axis=3, tiled=True)),
            "slab",
            split_axis=3,
            concat_axis=2,
            tiled=True,
        )
        return contract("nckxy,cdkz->ndxyz", planes, inverse_pair)

    pair_bits = pair_mask[0]
    own_group = lax.axis_index("grp")
    partner_group = jnp.bitwise_xor(own_group, pair_bits)
    upper_side = (own_group > partner_group).astype(jnp.int32)
    weights = 0.25 * occupation.astype(jnp.float32)
    level_count = lax.axis_size("grp").bit_length() - 1
    theirs = orbitals
    their_weights = weights
    for bit_level in range(level_count):
        arrived = swapped((theirs, their_weights), "grp", bit_level)
        chosen_flag = jnp.bitwise_and(jnp.right_shift(pair_bits, bit_level), 1) == 1
        theirs = jnp.where(chosen_flag, arrived[0], theirs)
        their_weights = jnp.where(chosen_flag, arrived[1], their_weights)
    paired = theirs.reshape(half_count, 2, plane_count, grid_len * grid_len)
    paired_weights = their_weights.reshape(half_count, 2)

    def add_returned(returned, parity, term):
        current = lax.dynamic_slice_in_dim(returned, parity, 1, 1)
        return lax.dynamic_update_slice_in_dim(returned, current + term[:, None], parity, 1)

    def twin_step(pair_number, loop_state):
        kept_rows, returned = loop_state
        first_row = 2 * pair_number
        second_row = first_row + 1
        own_first = lax.dynamic_index_in_dim(orbitals, first_row, 0, keepdims=False)
        own_second = lax.dynamic_index_in_dim(orbitals, second_row, 0, keepdims=False)
        weight_first = lax.dynamic_index_in_dim(weights, first_row, 0, keepdims=False)
        weight_second = lax.dynamic_index_in_dim(weights, second_row, 0, keepdims=False)
        parity_first = upper_side % 2
        parity_second = 1 - parity_first
        chosen_first = lax.dynamic_index_in_dim(paired, parity_first, 1, keepdims=False)
        chosen_second = lax.dynamic_index_in_dim(paired, parity_second, 1, keepdims=False)
        cweight_first = lax.dynamic_index_in_dim(paired_weights, parity_first, 1, keepdims=False)
        cweight_second = lax.dynamic_index_in_dim(paired_weights, parity_second, 1, keepdims=False)
        density_pair = jnp.stack(
            [own_first[None] * chosen_first, own_second[None] * chosen_second], axis=1
        )
        density_pair = density_pair.reshape(half_count, 2, plane_count, grid_len, grid_len)
        fields = packed_potential(density_pair).reshape(
            half_count, 2, plane_count, grid_len * grid_len
        )
        field_first = fields[:, 0]
        field_second = fields[:, 1]
        kept_first = -jnp.sum(cweight_first[:, None, None] * field_first * chosen_first, axis=0)
        kept_second = -jnp.sum(cweight_second[:, None, None] * field_second * chosen_second, axis=0)
        kept_rows = lax.dynamic_update_index_in_dim(kept_rows, kept_first, first_row, 0)
        kept_rows = lax.dynamic_update_index_in_dim(kept_rows, kept_second, second_row, 0)
        returned = add_returned(
            returned, parity_first, -weight_first * field_first * own_first[None]
        )
        returned = add_returned(
            returned, parity_second, -weight_second * field_second * own_second[None]
        )
        return (kept_rows, returned)

    kept_start = jnp.zeros(orbitals.shape, jnp.float32)
    returned_start = jnp.zeros((half_count, 2, plane_count, grid_len * grid_len), jnp.float32)
    kept_rows, returned = lax.fori_loop(0, half_count, twin_step, (kept_start, returned_start))
    outgoing = returned.reshape(orbit_count, plane_count, grid_len * grid_len)
    incoming = outgoing
    for bit_level in range(level_count):
        arrived_terms = swapped(incoming, "grp", bit_level)
        chosen_flag = jnp.bitwise_and(jnp.right_shift(pair_bits, bit_level), 1) == 1
        incoming = jnp.where(chosen_flag, arrived_terms, incoming)
    return kept_rows + incoming


def solution(mesh):
    return jax.shard_map(
        local,
        mesh=mesh,
        in_specs=(P("grp", "slab", None), P("grp"), P("slab", None), P()),
        out_specs=P("grp", "slab", None),
        check_vma=False,
    )
```

profile of v0, /device:TPU:0, one launch (start us, length us, event | category | flops | bytes accessed | tf_op | source)
XLA Modules:
  0.0 155.2 jit_solution(10319154145023232211)
XLA Ops:
  0.0 1.7 %collective-permute-start.3 = (f32[2,6,9216]{2,0,1:T(2,128)}, f32[2,6,9216]{2,0,1:T(2,128)S(1)}, u32[]{:S(2)}, u32[]{:S(2)}) collective-permute-start(f32[2,6,9216]{2,0,1:T(2,128)} %param.4), channel_id=1, source_target_pairs={{0,16},{16,0},{32,48},{48,32},{64,80},{80,64},{96,112},{112,96},{1... | collective-permute-start | bytes 1327112 | tf_op jit(solution)/shard_map/ppermute | solution.py:14
  2.4 9.7 %collective-permute-done.3 = f32[2,6,9216]{2,0,1:T(2,128)S(1)} collective-permute-done((f32[2,6,9216]{2,0,1:T(2,128)}, f32[2,6,9216]{2,0,1:T(2,128)S(1)}, u32[]{:S(2)}, u32[]{:S(2)}) %collective-permute-start.3) | collective-permute-done | bytes 442400 | tf_op jit(solution)/shard_map/ppermute | solution.py:14
  12.1 1.2 broadcast_select_fusion.1
  13.3 2.2 %collective-permute-start.4 = (f32[2,6,9216]{2,0,1:T(2,128)S(1)}, f32[2,6,9216]{2,0,1:T(2,128)S(1)}, u32[]{:S(2)}, u32[]{:S(2)}) collective-permute-start(f32[2,6,9216]{2,0,1:T(2,128)S(1)} %broadcast_select_fusion.1), channel_id=1, source_target_pairs={{0,32},{16,48},{32,0},{48,16},{64,96},{80,112},{96,64},{112,80},{1... | collective-permute-start | bytes 1327112 | tf_op jit(solution)/shard_map/ppermute | solution.py:14
  15.5 9.3 %collective-permute-done.4 = f32[2,6,9216]{2,0,1:T(2,128)S(1)} collective-permute-done((f32[2,6,9216]{2,0,1:T(2,128)S(1)}, f32[2,6,9216]{2,0,1:T(2,128)S(1)}, u32[]{:S(2)}, u32[]{:S(2)}) %collective-permute-start.4) | collective-permute-done | bytes 442400 | tf_op jit(solution)/shard_map/ppermute | solution.py:14
  24.8 0.2 broadcast_select_fusion.3
  25.0 3.8 %collective-permute-start.5 = (f32[2,6,9216]{2,0,1:T(2,128)S(1)}, f32[2,6,9216]{2,0,1:T(2,128)S(1)}, u32[]{:S(2)}, u32[]{:S(2)}) collective-permute-start(f32[2,6,9216]{2,0,1:T(2,128)S(1)} %broadcast_select_fusion.3), channel_id=1, source_target_pairs={{0,64},{16,80},{32,96},{48,112},{64,0},{80,16},{96,32},{112,48},{1... | collective-permute-start | bytes 1327112 | tf_op jit(solution)/shard_map/ppermute | solution.py:14
  28.8 0.4 fusion.40
  29.2 0.4 fusion.33
  29.7 7.9 %collective-permute-done.5 = f32[2,6,9216]{2,0,1:T(2,128)S(1)} collective-permute-done((f32[2,6,9216]{2,0,1:T(2,128)S(1)}, f32[2,6,9216]{2,0,1:T(2,128)S(1)}, u32[]{:S(2)}, u32[]{:S(2)}) %collective-permute-start.5) | collective-permute-done | bytes 442400 | tf_op jit(solution)/shard_map/ppermute | solution.py:14
  37.6 0.2 broadcast_select_fusion.4
  37.8 0.0 copy-start.3
  37.8 1.4 multiply_reduce_fusion.1
  39.3 0.1 stack.60
  39.4 0.1 stack.61
  39.5 1.2 convolution_bitcast_fusion
  40.7 0.0 copy-done.5
  40.7 0.0 copy-done.7
  40.7 1.9 %copy.50 = f32[1,2,192,6,96]{4,1,3,0,2:T(2,128)} copy(f32[1,2,192,6,96]{4,2,3,1,0:T(8,128)S(1)} %convolution_bitcast_fusion) | data formatting | bytes 1769472 | tf_op jit(solution)/shard_map/while/body/eval_jaxpr/ncxyz,cdzk->ndkxy/transpose | solution.py:25
  42.7 7.0 %all-to-all-start = ((f32[1,2,192,6,96]{4,1,3,0,2:T(2,128)}), f32[1,2,192,6,96]{4,1,3,0,2:T(2,128)S(1)}, u32[]{:S(2)}, u32[]{:S(2)}) async-start(f32[1,2,192,6,96]{4,1,3,0,2:T(2,128)} %copy.50), calls=%async_computation | async-start | bytes 2359296 | tf_op jit(solution)/shard_map/while/body/eval_jaxpr/all_to_all | solution.py:54
  49.7 2.3 %mul.246 = f32[12,192,192]{2,1,0:T(8,128)S(1)} reshape(f32[12,36864]{1,0:T(8,128)} %param.6) | data formatting | bytes 3538944 | tf_op jit(solution)/shard_map/while/body/eval_jaxpr/mul | solution.py:47
  52.1 2.1 %copy.54 = f32[12,192,192]{1,2,0:T(8,128)} copy(f32[12,192,192]{2,1,0:T(8,128)S(1)} %mul.246) | data formatting | bytes 3538944 | tf_op jit(solution)/shard_map/while/body/eval_jaxpr/mul | solution.py:47
  54.2 0.4 fusion.39
  54.6 0.4 sine_multiply_fusion
  55.0 14.0 %all-to-all-done = f32[1,2,192,6,96]{4,1,3,0,2:T(2,128)S(1)} async-done(((f32[1,2,192,6,96]{4,1,3,0,2:T(2,128)}), f32[1,2,192,6,96]{4,1,3,0,2:T(2,128)S(1)}, u32[]{:S(2)}, u32[]{:S(2)}) %all-to-all-start) | async-done | bytes 884768 | tf_op jit(solution)/shard_map/while/body/eval_jaxpr/all_to_all | solution.py:54
  69.1 0.5 copy.51
  69.6 2.1 %fusion.12 = f32[2,192,12,96,1]{3,1,4,2,0:T(8,128)S(1)} fusion(f32[2,12,96,96]{3,0,2,1:T(2,128)S(1)} %bitcast.166, f32[1,2,96,192]{2,3,0,1:T(8,128)S(1)} %copy-done.8, f32[1,2,96,192]{2,3,0,1:T(8,128)S(1)} %copy-done.6), kind=kOutput, calls=%fused_computation.12 | convolution fusion | flops 1019289600 | bytes 2949120 | tf_op jit(solution)/shard_map/while/body/eval_jaxpr/nckxy,cdyl->ndkxl/dot_general | solution.py:25
  71.8 3.9 %fusion.5 = f32[2,192,12,192,1]{3,1,2,4,0:T(8,128)S(1)} fusion(f32[2,192,12,96,1]{3,1,4,2,0:T(8,128)S(1)} %fusion.12, f32[1,2,96,192]{2,3,0,1:T(8,128)S(1)} %copy-done.8, f32[1,2,96,192]{2,3,0,1:T(8,128)S(1)} %copy-done.6), kind=kOutput, calls=%fused_computation.5 | convolution fusion | flops 2038505472 | bytes 5603328 | tf_op jit(solution)/shard_map/while/body/eval_jaxpr/nckxl,cdxm->ndklm/dot_general | solution.py:25
  75.7 4.0 %fusion.1 = f32[2,96,12,192,1]{3,1,2,4,0:T(8,128)S(1)} fusion(f32[2,192,12,192,1]{3,1,2,4,0:T(8,128)S(1)} %fusion.5, f32[12,192,192]{1,2,0:T(8,128)S(1)} %copy-done, f32[1,2,192,96]{2,3,0,1:T(8,128)S(1)} %get-tuple-element.32, f32[1,2,192,96]{2,3,0,1:T(8,128)S(1)} %get-tuple-element.31), kind=kOutput, calls=%fused_computation.2 | convolution fusion | flops 2039390208 | bytes 7372800 | tf_op jit(solution)/shard_map/while/body/eval_jaxpr/ncklm,cdmx->ndklx/dot_general | solution.py:25
  79.7 3.0 %fusion.8 = f32[1,2,12,96,96]{3,4,2,1,0:T(8,128)S(1)} fusion(f32[2,96,12,192,1]{3,1,2,4,0:T(8,128)S(1)} %fusion.1, f32[1,2,192,96]{2,3,0,1:T(8,128)S(1)} %get-tuple-element.32, f32[1,2,192,96]{2,3,0,1:T(8,128)S(1)} %get-tuple-element.31), kind=kOutput, calls=%fused_computation.8 | convolution fusion | flops 1019289600 | bytes 2949120 | tf_op jit(solution)/shard_map/while/body/eval_jaxpr/ncklx,cdly->ndkxy/dot_general | solution.py:25
  82.7 0.0 copy-start.9
  82.7 1.4 copy.57
  84.1 3.7 %all-to-all-start.1 = ((f32[1,2,12,96,96]{4,1,2,0,3:T(2,128)}), f32[1,2,12,96,96]{4,1,2,0,3:T(2,128)S(1)}, u32[]{:S(2)}, u32[]{:S(2)}) async-start(f32[1,2,12,96,96]{4,1,2,0,3:T(2,128)} %copy.57), calls=%async_computation.1 | async-start | bytes 2359296 | tf_op jit(solution)/shard_map/while/body/eval_jaxpr/all_to_all | solution.py:53
  87.8 0.6 fusion.47
  89.7 17.5 %all-to-all-done.1 = f32[1,2,12,96,96]{4,1,2,0,3:T(2,128)S(1)} async-done(((f32[1,2,12,96,96]{4,1,2,0,3:T(2,128)}), f32[1,2,12,96,96]{4,1,2,0,3:T(2,128)S(1)}, u32[]{:S(2)}, u32[]{:S(2)}) %all-to-all-start.1) | async-done | bytes 884768 | tf_op jit(solution)/shard_map/while/body/eval_jaxpr/all_to_all | solution.py:53
  107.1 0.5 copy.58
  107.7 0.4 copy.59
  108.1 0.0 copy-start.2
  108.1 1.2 convolution_bitcast_fusion.1
  109.3 0.2 copy.61
  109.5 0.6 reshape.235
  110.1 0.2 broadcast_in_dim.25
  110.4 0.3 bitcast_dynamic-update-slice_fusion
  110.6 0.0 copy-start.4
  110.7 0.2 copy.92
  110.9 0.5 fusion.24
  111.4 4.7 %dynamic_update_slice.18 = f32[2,6,9216]{2,0,1:T(2,128)S(1)} dynamic-update-slice(f32[2,6,9216]{2,0,1:T(2,128)S(1)} %bitcast.167, f32[1,6,9216]{2,0,1:T(1,128)S(1)} %fusion.24, s32[]{:T(128)S(6)} %select_n.158, s32[]{:T(128)} %constant.85.clone.1, s32[]{:T(128)} %constant.85.clone.1) | dynamic-update-slice | bytes 442372 | tf_op jit(solution)/shard_map/while/body/eval_jaxpr/dynamic_update_slice | solution.py:80
  116.1 0.7 collective-permute-start.6
  116.8 1.4 collective-permute-start
  118.2 9.9 %collective-permute-done = f32[2]{0:T(128)S(1)} collective-permute-done((f32[2]{0:T(128)S(1)}, f32[2]{0:T(128)S(1)}, u32[]{:S(2)}, u32[]{:S(2)}) %collective-permute-start) | collective-permute-done | bytes 40 | tf_op jit(solution)/shard_map/ppermute | solution.py:14
  128.1 1.0 collective-permute-start.1
  129.0 0.0 collective-permute-done.6
  129.0 0.2 broadcast_select_fusion
  129.3 1.1 collective-permute-start.7
  130.4 1.2 collective-permute-done.1
  131.6 2.9 %collective-permute-start.2 = (f32[2]{0:T(128)S(1)}, f32[2]{0:T(128)S(1)}, u32[]{:S(2)}, u32[]{:S(2)}) collective-permute-start(f32[2]{0:T(128)S(1)} %broadcast_select_fusion.6), channel_id=1, source_target_pairs={{0,64},{16,80},{32,96},{48,112},{64,0},{80,16},{96,32},{112,48},{1... | collective-permute-start | bytes 32 | tf_op jit(solution)/shard_map/ppermute | solution.py:14
  134.5 7.3 %collective-permute-done.2 = f32[2]{0:T(128)S(1)} collective-permute-done((f32[2]{0:T(128)S(1)}, f32[2]{0:T(128)S(1)}, u32[]{:S(2)}, u32[]{:S(2)}) %collective-permute-start.2) | collective-permute-done | bytes 40 | tf_op jit(solution)/shard_map/ppermute | solution.py:14
  141.9 0.7 fusion.48
  142.6 0.0 collective-permute-done.7
  142.6 0.2 broadcast_select_fusion.2
  142.8 1.0 collective-permute-start.8
  143.8 1.9 %fusion.26 = (f32[1,6,9216]{2,0,1:T(1,128)S(1)}, f32[1,6,9216]{2,0,1:T(1,128)S(1)}) fusion(f32[1,2,6,9216]{3,1,2,0:T(2,128)S(1)} %reshape.235, f32[2,6,9216]{2,0,1:T(2,128)S(1)} %copy-done.4, s32[]{:T(128)S(6)} %select_n.149, f32[]{:T(128)} %bitcast.1, s32[]{:T(128)S(6)} %select_n.158, f32[]{:T(128)} %bitcast.54), kind=kLoop, calls=%fused_computation.44 | loop fusion | flops 331776 | bytes 1327120 | tf_op jit(solution)/shard_map/while/body/eval_jaxpr/neg | solution.py:105
  145.8 8.1 %collective-permute-done.8 = f32[2,6,9216]{2,0,1:T(2,128)S(1)} collective-permute-done((f32[2,6,9216]{2,0,1:T(2,128)S(1)}, f32[2,6,9216]{2,0,1:T(2,128)S(1)}, u32[]{:S(2)}, u32[]{:S(2)}) %collective-permute-start.8) | collective-permute-done | bytes 442400 | tf_op jit(solution)/shard_map/ppermute | solution.py:14
  153.8 1.3 maximum_add_fusion
  (20 shorter events, 0.1 us)
Async XLA Ops:
  0.0 12.1 %collective-permute-start.3 = (f32[2,6,9216]{2,0,1:T(2,128)}, f32[2,6,9216]{2,0,1:T(2,128)S(1)}, u32[]{:S(2)}, u32[]{:S(2)}) collective-permute-start(f32[2,6,9216]{2,0,1:T(2,128)} %param.4), channel_id=1, source_target_pairs={{0,16},{16,0},{32,48},{48,32},{64,80},{80,64},{96,112},{112,96},{1... | collective-permute-start | bytes 1327112 | tf_op jit(solution)/shard_map/ppermute | solution.py:14
  2.3 35.5 %copy-start.1 = (f32[2,6,9216]{2,0,1:T(2,128)S(1)}, f32[2,6,9216]{2,0,1:T(2,128)}, u32[]{:S(2)}) copy-start(f32[2,6,9216]{2,0,1:T(2,128)} %param.4) | copy-start | bytes 1327108
  13.3 11.5 %collective-permute-start.4 = (f32[2,6,9216]{2,0,1:T(2,128)S(1)}, f32[2,6,9216]{2,0,1:T(2,128)S(1)}, u32[]{:S(2)}, u32[]{:S(2)}) collective-permute-start(f32[2,6,9216]{2,0,1:T(2,128)S(1)} %broadcast_select_fusion.1), channel_id=1, source_target_pairs={{0,32},{16,48},{32,0},{48,16},{64,96},{80,112},{96,64},{112,80},{1... | collective-permute-start | bytes 1327112 | tf_op jit(solution)/shard_map/ppermute | solution.py:14
  25.0 12.5 %collective-permute-start.5 = (f32[2,6,9216]{2,0,1:T(2,128)S(1)}, f32[2,6,9216]{2,0,1:T(2,128)S(1)}, u32[]{:S(2)}, u32[]{:S(2)}) collective-permute-start(f32[2,6,9216]{2,0,1:T(2,128)S(1)} %broadcast_select_fusion.3), channel_id=1, source_target_pairs={{0,64},{16,80},{32,96},{48,112},{64,0},{80,16},{96,32},{112,48},{1... | collective-permute-start | bytes 1327112 | tf_op jit(solution)/shard_map/ppermute | solution.py:14
  29.7 11.1 %copy-start.5 = (f32[1,2,96,192]{2,3,0,1:T(8,128)}, f32[1,2,96,192]{2,3,0,1:T(8,128)S(1)}, u32[]{:S(2)}) copy-start(f32[1,2,96,192]{2,3,0,1:T(8,128)S(1)} %get-tuple-element.33) | copy-start | bytes 442372
  29.7 11.1 %copy-start.7 = (f32[1,2,96,192]{2,3,0,1:T(8,128)}, f32[1,2,96,192]{2,3,0,1:T(8,128)S(1)}, u32[]{:S(2)}) copy-start(f32[1,2,96,192]{2,3,0,1:T(8,128)S(1)} %get-tuple-element.34) | copy-start | bytes 442372
  37.8 1.5 copy-start.3
  42.7 26.4 %all-to-all-start = ((f32[1,2,192,6,96]{4,1,3,0,2:T(2,128)}), f32[1,2,192,6,96]{4,1,3,0,2:T(2,128)S(1)}, u32[]{:S(2)}, u32[]{:S(2)}) async-start(f32[1,2,192,6,96]{4,1,3,0,2:T(2,128)} %copy.50), calls=%async_computation | async-start | bytes 2359296 | tf_op jit(solution)/shard_map/while/body/eval_jaxpr/all_to_all | solution.py:54
  54.2 15.5 %copy-start.6 = (f32[1,2,96,192]{2,3,0,1:T(8,128)S(1)}, f32[1,2,96,192]{2,3,0,1:T(8,128)}, u32[]{:S(2)}) copy-start(f32[1,2,96,192]{2,3,0,1:T(8,128)} %copy-done.5) | copy-start | bytes 442372
  54.2 15.5 %copy-start.8 = (f32[1,2,96,192]{2,3,0,1:T(8,128)S(1)}, f32[1,2,96,192]{2,3,0,1:T(8,128)}, u32[]{:S(2)}) copy-start(f32[1,2,96,192]{2,3,0,1:T(8,128)} %copy-done.7) | copy-start | bytes 442372
  71.7 3.9 %copy-start = (f32[12,192,192]{1,2,0:T(8,128)S(1)}, f32[12,192,192]{1,2,0:T(8,128)}, u32[]{:S(2)}) copy-start(f32[12,192,192]{1,2,0:T(8,128)} %copy.54) | copy-start | bytes 5308420
  82.7 5.1 %copy-start.9 = (s32[2]{0:T(128)S(1)}, s32[2]{0:T(128)}, u32[]{:S(2)}) copy-start(s32[2]{0:T(128)} %param.5) | copy-start | bytes 28
  84.1 23.0 %all-to-all-start.1 = ((f32[1,2,12,96,96]{4,1,2,0,3:T(2,128)}), f32[1,2,12,96,96]{4,1,2,0,3:T(2,128)S(1)}, u32[]{:S(2)}, u32[]{:S(2)}) async-start(f32[1,2,12,96,96]{4,1,2,0,3:T(2,128)} %copy.57), calls=%async_computation.1 | async-start | bytes 2359296 | tf_op jit(solution)/shard_map/while/body/eval_jaxpr/all_to_all | solution.py:53
  108.1 2.3 %copy-start.2 = (f32[2,6,9216]{2,0,1:T(2,128)S(1)}, f32[2,6,9216]{2,0,1:T(2,128)}, u32[]{:S(2)}) copy-start(f32[2,6,9216]{2,0,1:T(2,128)} %param.4) | copy-start | bytes 1327108
  110.6 33.2 %copy-start.4 = (f32[2,6,9216]{2,0,1:T(2,128)S(1)}, f32[2,6,9216]{2,0,1:T(2,128)}, u32[]{:S(2)}) copy-start(f32[2,6,9216]{2,0,1:T(2,128)} %copy-done.3) | copy-start | bytes 1327108
  116.1 13.0 %collective-permute-start.6 = (f32[2,6,9216]{2,0,1:T(2,128)S(1)}, f32[2,6,9216]{2,0,1:T(2,128)S(1)}, u32[]{:S(2)}, u32[]{:S(2)}) collective-permute-start(f32[2,6,9216]{2,0,1:T(2,128)S(1)} %dynamic_update_slice.18), channel_id=1, source_target_pairs={{0,16},{16,0},{32,48},{48,32},{64,80},{80,64},{96,112},{112,96},{1... | collective-permute-start | bytes 1327112 | tf_op jit(solution)/shard_map/ppermute | solution.py:14
  116.8 11.2 %collective-permute-start = (f32[2]{0:T(128)S(1)}, f32[2]{0:T(128)S(1)}, u32[]{:S(2)}, u32[]{:S(2)}) collective-permute-start(f32[2]{0:T(128)S(1)} %convert_multiply_fusion), channel_id=1, source_target_pairs={{0,16},{16,0},{32,48},{48,32},{64,80},{80,64},{96,112},{112,96},{1... | collective-permute-start | bytes 32 | tf_op jit(solution)/shard_map/ppermute | solution.py:14
  128.1 3.6 %collective-permute-start.1 = (f32[2]{0:T(128)S(1)}, f32[2]{0:T(128)S(1)}, u32[]{:S(2)}, u32[]{:S(2)}) collective-permute-start(f32[2]{0:T(128)S(1)} %broadcast_select_fusion.5), channel_id=1, source_target_pairs={{0,32},{16,48},{32,0},{48,16},{64,96},{80,112},{96,64},{112,80},{1... | collective-permute-start | bytes 32 | tf_op jit(solution)/shard_map/ppermute | solution.py:14
  129.3 13.3 %collective-permute-start.7 = (f32[2,6,9216]{2,0,1:T(2,128)S(1)}, f32[2,6,9216]{2,0,1:T(2,128)S(1)}, u32[]{:S(2)}, u32[]{:S(2)}) collective-permute-start(f32[2,6,9216]{2,0,1:T(2,128)S(1)} %broadcast_select_fusion), channel_id=1, source_target_pairs={{0,32},{16,48},{32,0},{48,16},{64,96},{80,112},{96,64},{112,80},{1... | collective-permute-start | bytes 1327112 | tf_op jit(solution)/shard_map/ppermute | solution.py:14
  131.6 10.3 %collective-permute-start.2 = (f32[2]{0:T(128)S(1)}, f32[2]{0:T(128)S(1)}, u32[]{:S(2)}, u32[]{:S(2)}) collective-permute-start(f32[2]{0:T(128)S(1)} %broadcast_select_fusion.6), channel_id=1, source_target_pairs={{0,64},{16,80},{32,96},{48,112},{64,0},{80,16},{96,32},{112,48},{1... | collective-permute-start | bytes 32 | tf_op jit(solution)/shard_map/ppermute | solution.py:14
  142.8 11.0 %collective-permute-start.8 = (f32[2,6,9216]{2,0,1:T(2,128)S(1)}, f32[2,6,9216]{2,0,1:T(2,128)S(1)}, u32[]{:S(2)}, u32[]{:S(2)}) collective-permute-start(f32[2,6,9216]{2,0,1:T(2,128)S(1)} %broadcast_select_fusion.2), channel_id=1, source_target_pairs={{0,64},{16,80},{32,96},{48,112},{64,0},{80,16},{96,32},{112,48},{1... | collective-permute-start | bytes 1327112 | tf_op jit(solution)/shard_map/ppermute | solution.py:14
where the time goes:
time: 156 us; the launch traced here: 155 us
  waiting for transfers between devices  84.9 us (54%)
  starting transfers between devices  26.5 us (17%)
  local copies, waits for them, and re-layouts  16.8 us (11%)
  matrix products  15.4 us (10%)
  other arithmetic  9.36 us (6%)
  between operations  2.21 us (1%)
    ppermute x9, waiting for transfers between devices, swapped(): return lax.ppermute(value, axis, pairs)  53.4 us
    all_to_all x1, waiting for transfers between devices, packed_potential(): lax.all_to_all(line_work(lax.all_to_all(spread, 'slab', split_axis=2, con...  17.5 us
    ppermute x9, starting transfers between devices, swapped(): return lax.ppermute(value, axis, pairs)  15.8 us
    dot_general x6, matrix products, contract(): jnp.einsum(form, left, right, precision=lax.Precision.HIGHEST, preferred_...  15.4 us
    all_to_all x1, waiting for transfers between devices, packed_potential(): lax.all_to_all(spread, 'slab', split_axis=2, concat_axis=3, tiled=True)  14 us
    all_to_all x1, starting transfers between devices, packed_potential(): lax.all_to_all(spread, 'slab', split_axis=2, concat_axis=3, tiled=True)  7.03 us
    dynamic_update_slice x2, local copies, waits for them, and re-layouts, add_returned(): lax.dynamic_update_slice_in_dim(returned, current + term[:, None], parity...  4.88 us
    mul x2, local copies, waits for them, and re-layouts, line_work(): spectra = spectra * kernel_cube[None, None]  4.45 us
  transfers between devices with their start and end apart: 11, of which 9 were waited for; matrix products, arithmetic and copies ran while one was open for 6% of the time, Pallas kernels for 0%

commit v1 on v0

v1 whole, which is shorter than its diff:
```python
import math

import jax
import jax.numpy as jnp
from jax import lax
from jax.sharding import PartitionSpec as P

G = 96


def to_partner(value, pair_bits):
    group_count = lax.axis_size("grp")

    def by_mask(mask):
        pairs = [(source, source ^ mask) for source in range(group_count)]
        return lambda sent: lax.ppermute(sent, "grp", pairs)

    branches = [by_mask(mask) for mask in range(1, group_count)]
    return lax.switch(pair_bits - 1, branches, value)


def dft_tables(size_in, size_out, period):
    row_index = lax.broadcasted_iota(jnp.int32, (size_in, size_out), 0)
    col_index = lax.broadcasted_iota(jnp.int32, (size_in, size_out), 1)
    phase_angle = (row_index * col_index % period).astype(jnp.float32) * (2.0 * math.pi / period)
    return (jnp.cos(phase_angle), jnp.sin(phase_angle))


def contract(form, left, right):
    return jnp.einsum(
        form, left, right, precision=lax.Precision.HIGH, preferred_element_type=jnp.float32
    )


def local(orbitals, occupation, kernel_hat, pair_mask):
    orbit_count = orbitals.shape[0]
    half_count = orbit_count // 2
    plane_count = orbitals.shape[1]
    grid_len = G
    padded_len = 2 * G
    kernel_cube = kernel_hat.reshape(kernel_hat.shape[0], padded_len, padded_len)
    cos_fwd, sin_fwd = dft_tables(grid_len, padded_len, padded_len)
    cos_inv, sin_inv = dft_tables(padded_len, grid_len, padded_len)
    cos_inv = cos_inv / padded_len
    sin_inv = sin_inv / padded_len
    forward_pair = jnp.stack([jnp.stack([cos_fwd, -sin_fwd]), jnp.stack([sin_fwd, cos_fwd])])
    inverse_pair = jnp.stack([jnp.stack([cos_inv, sin_inv]), jnp.stack([-sin_inv, cos_inv])])

    def line_work(pencils):
        y_spectra = contract("nckxy,cdyl->ndkxl", pencils, forward_pair)
        spectra = contract("nckxl,cdxm->ndklm", y_spectra, forward_pair)
        spectra = spectra * kernel_cube[None, None]
        x_back = contract("ncklm,cdmx->ndklx", spectra, inverse_pair)
        return contract("ncklx,cdly->ndkxy", x_back, inverse_pair)

    def packed_potential(density_pair):
        spread = contract("ncxyz,cdzk->ndkxy", density_pair, forward_pair)
        planes = lax.all_to_all(
            line_work(lax.all_to_all(spread, "slab", split_axis=2, concat_axis=3, tiled=True)),
            "slab",
            split_axis=3,
            concat_axis=2,
            tiled=True,
        )
        return contract("nckxy,cdkz->ndxyz", planes, inverse_pair)

    pair_bits = pair_mask[0]
    own_group = lax.axis_index("grp")
    partner_group = jnp.bitwise_xor(own_group, pair_bits)
    upper_side = (own_group > partner_group).astype(jnp.int32)
    weights = 0.25 * occupation.astype(jnp.float32)
    root_weights = jnp.sqrt(weights)
    scaled = orbitals * root_weights[:, None, None]
    theirs = to_partner(scaled, pair_bits)
    paired = theirs
    first = jnp.where(upper_side == 1, theirs[1], theirs[0])
    second = jnp.where(upper_side == 1, theirs[0], theirs[1])
    density_pair = jnp.stack([scaled[0] * first, scaled[1] * second])[None]
    density_pair = density_pair.reshape(half_count, 2, plane_count, grid_len, grid_len)
    fields = packed_potential(density_pair).reshape(2, plane_count, grid_len * grid_len)
    kept_rows = jnp.stack([fields[0] * first, fields[1] * second])
    sent_first = fields[0] * scaled[0]
    sent_second = fields[1] * scaled[1]
    outgoing = jnp.stack(
        [
            jnp.where(upper_side == 1, sent_second, sent_first),
            jnp.where(upper_side == 1, sent_first, sent_second),
        ]
    )
    incoming = to_partner(outgoing, pair_bits)
    return (kept_rows + incoming) * (-1.0 / root_weights)[:, None, None]


def solution(mesh):
    return jax.shard_map(
        local,
        mesh=mesh,
        in_specs=(P("grp", "slab", None), P("grp"), P("slab", None), P()),
        out_specs=P("grp", "slab", None),
        check_vma=False,
    )
```

time: 156 us -> 101 us (0.65); the launches traced: 155 us -> 102 us
  waiting for transfers between devices: 84.9 us -> 34.8 us
  blocking collectives: 0 us -> 21.7 us
  starting transfers between devices: 26.5 us -> 14.4 us
  matrix products: 15.4 us -> 8.18 us
  local copies, waits for them, and re-layouts: 16.8 us -> 10.7 us
  other arithmetic: 9.36 us -> 11.3 us
    ppermute x9 -> x2, waiting for transfers between devices: 53.4 us -> 20.8 us  [by_mask(): return lambda sent: lax.ppermute(sent, 'grp', pairs)]
    all_to_all x0 -> x1, blocking collectives: none -> 21.7 us  [packed_potential(): lax.all_to_all(line_work(lax.all_to_all(spread, 'slab', split_axis=2, con...]
    all_to_all x1 -> x0, waiting for transfers between devices: 17.5 us -> none  [packed_potential(): lax.all_to_all(line_work(lax.all_to_all(spread, 'slab', split_axis=2, con...]
    ppermute x9 -> x2, starting transfers between devices: 15.8 us -> 7.39 us  [by_mask(): return lambda sent: lax.ppermute(sent, 'grp', pairs)]
    dot_general x6, matrix products: 15.4 us -> 8.18 us  [contract(): jnp.einsum(form, left, right, precision=lax.Precision.HIGH, preferred_ele...]
    mul x2 -> x4, other arithmetic: 1.44 us -> 8.5 us  [the longest x1 2.88 us: local(): density_pair = jnp.stack([scaled[0] * first, scaled[1] * second])[None]]
    dynamic_update_slice x2 -> x0, local copies, waits for them, and re-layouts: 4.88 us -> none  [add_returned(): lax.dynamic_update_slice_in_dim(returned, current + term[:, None], parity...]
    all_to_all x1 -> x0, starting transfers between devices: 3.7 us -> none  [packed_potential(): lax.all_to_all(line_work(lax.all_to_all(spread, 'slab', split_axis=2, con...]
  transfers between devices with their start and end apart: 11 -> 3, of which waited for: 9 -> 3; matrix products, arithmetic and copies ran while one was open for 6% -> 5% of each run, Pallas kernels for 0% -> 0%
where the time goes in v1:
time: 101 us; the launch traced here: 102 us
  waiting for transfers between devices  34.8 us (34%)
  blocking collectives  21.7 us (21%)
  starting transfers between devices  14.4 us (14%)
  other arithmetic  11.3 us (11%)
  local copies, waits for them, and re-layouts  10.7 us (11%)
  matrix products  8.18 us (8%)
    all_to_all x1, blocking collectives, packed_potential(): lax.all_to_all(line_work(lax.all_to_all(spread, 'slab', split_axis=2, con...  21.7 us
    ppermute x2, waiting for transfers between devices, by_mask(): return lambda sent: lax.ppermute(sent, 'grp', pairs)  20.8 us
    all_to_all x1, waiting for transfers between devices, packed_potential(): lax.all_to_all(spread, 'slab', split_axis=2, concat_axis=3, tiled=True)  14 us
    dot_general x6, matrix products, contract(): jnp.einsum(form, left, right, precision=lax.Precision.HIGH, preferred_ele...  8.18 us
    ppermute x2, starting transfers between devices, by_mask(): return lambda sent: lax.ppermute(sent, 'grp', pairs)  7.39 us
    all_to_all x1, starting transfers between devices, packed_potential(): lax.all_to_all(spread, 'slab', split_axis=2, concat_axis=3, tiled=True)  7.04 us
    mul x2, local copies, waits for them, and re-layouts, line_work(): spectra = spectra * kernel_cube[None, None]  4.47 us
    mul x1, other arithmetic, local(): density_pair = jnp.stack([scaled[0] * first, scaled[1] * second])[None]  2.88 us
  transfers between devices with their start and end apart: 3, of which 3 were waited for; matrix products, arithmetic and copies ran while one was open for 5% of the time, Pallas kernels for 0%

profile of v1, /device:TPU:0, one launch (start us, length us, event | category | flops | bytes accessed | tf_op | source)
XLA Modules:
  0.0 102.1 jit_solution(14554560056412928326)
XLA Ops:
  0.0 0.4 fusion.38
  0.4 0.4 fusion.31
  1.5 0.7 broadcast_divide_fusion
  2.1 1.2 %broadcast_multiply_fusion = f32[2,6,9216]{2,0,1:T(2,128)S(1)} fusion(f32[2,6,9216]{2,0,1:T(2,128)} %param.18, f32[2]{0:T(128)S(1)} %get-tuple-element.56), kind=kLoop, calls=%fused_computation.34 | loop fusion | flops 110592 | bytes 884744 | tf_op jit(solution)/shard_map/mul | solution.py:73
  3.4 0.0 copy-start.1
  3.4 14.4 %conditional.2 = (f32[2,6,9216]{2,0,1:T(2,128)}) conditional(s32[]{:T(128)} %clamp.4, f32[2,6,9216]{2,0,1:T(2,128)S(1)} %broadcast_multiply_fusion, f32[2,6,9216]{2,0,1:T(2,128)S(1)} %broadcast_multiply_fusion, f32[2,6,9216]{2,0,1:T(2,128)S(1)} %broadcast_multiply_fusion, ...), branch_computations={%region_0.1_spmd, %region_1.2_spmd, %region_2.3_spmd, %region_3.4_... | conditional | bytes 1769520 | solution.py:19
  3.4 4.1 %collective-permute-start.3 = (f32[2,6,9216]{2,0,1:T(2,128)S(1)}, f32[2,6,9216]{2,0,1:T(2,128)}, u32[]{:S(2)}, u32[]{:S(2)}) collective-permute-start(f32[2,6,9216]{2,0,1:T(2,128)S(1)} %param.3), channel_id=1, source_target_pairs={{0,64},{16,80},{32,96},{48,112},{64,0},{80,16},{96,32},{112,48},{1... | collective-permute-start | bytes 1327112 | tf_op jit(solution)/shard_map/cond/branch_3_fun/ppermute | solution.py:16
  7.5 10.3 %collective-permute-done.3 = f32[2,6,9216]{2,0,1:T(2,128)} collective-permute-done((f32[2,6,9216]{2,0,1:T(2,128)S(1)}, f32[2,6,9216]{2,0,1:T(2,128)}, u32[]{:S(2)}, u32[]{:S(2)}) %collective-permute-start.3) | collective-permute-done | bytes 442400 | tf_op jit(solution)/shard_map/cond/branch_3_fun/ppermute | solution.py:16
  17.8 2.9 %multiply_reduce_fusion.1 = (f32[6,9216]{1,0:T(8,128)S(1)}, f32[6,9216]{1,0:T(8,128)S(1)}) fusion(f32[2,6,9216]{2,0,1:T(2,128)S(1)} %broadcast_multiply_fusion, f32[2,6,9216]{2,0,1:T(2,128)} %get-tuple-element.61, pred[]{:T(512)S(6)} %eq.6), kind=kLoop, calls=%fused_computation.36 | loop fusion | flops 221184 | bytes 1327105 | tf_op jit(solution)/shard_map/mul | solution.py:78
  20.7 0.1 stack.88
  20.8 0.1 stack.89
  20.9 0.0 copy-start.3
  21.0 0.0 copy-start.5
  21.0 0.7 copy-done.3
  21.6 0.1 copy-done.5
  21.7 0.7 convolution_bitcast_fusion
  22.4 0.0 copy-done.1
  22.4 1.9 %copy.85 = f32[1,2,192,6,96]{4,1,3,0,2:T(2,128)} copy(f32[1,2,192,6,96]{4,2,3,1,0:T(8,128)S(1)} %convolution_bitcast_fusion) | data formatting | bytes 1769472 | tf_op jit(solution)/shard_map/ncxyz,cdzk->ndkxy/transpose | solution.py:30
  24.3 7.0 %all-to-all-start = ((f32[1,2,192,6,96]{4,1,3,0,2:T(2,128)}), f32[1,2,192,6,96]{4,1,3,0,2:T(2,128)S(1)}, u32[]{:S(2)}, u32[]{:S(2)}) async-start(f32[1,2,192,6,96]{4,1,3,0,2:T(2,128)} %copy.85), calls=%async_computation | async-start | bytes 2359296 | tf_op jit(solution)/shard_map/all_to_all | solution.py:59
  31.4 2.3 %mul.189 = f32[12,192,192]{2,1,0:T(8,128)S(1)} reshape(f32[12,36864]{1,0:T(8,128)} %param.20) | data formatting | bytes 3538944 | tf_op jit(solution)/shard_map/mul | solution.py:52
  33.7 2.1 %copy.89 = f32[12,192,192]{1,2,0:T(8,128)} copy(f32[12,192,192]{2,1,0:T(8,128)S(1)} %mul.189) | data formatting | bytes 3538944 | tf_op jit(solution)/shard_map/mul | solution.py:52
  35.8 0.0 copy-start.4
  35.8 0.0 copy-start.6
  35.9 0.4 fusion.37
  36.2 0.4 sine_multiply_fusion
  36.7 0.0 copy-start.7
  36.7 0.0 copy-start.9
  36.7 14.0 %all-to-all-done = f32[1,2,192,6,96]{4,1,3,0,2:T(2,128)S(1)} async-done(((f32[1,2,192,6,96]{4,1,3,0,2:T(2,128)}), f32[1,2,192,6,96]{4,1,3,0,2:T(2,128)S(1)}, u32[]{:S(2)}, u32[]{:S(2)}) %all-to-all-start) | async-done | bytes 884768 | tf_op jit(solution)/shard_map/all_to_all | solution.py:59
  50.7 0.5 copy.86
  51.3 0.0 copy-done.4
  51.3 0.0 copy-done.6
  51.3 1.1 %fusion.12 = f32[2,192,12,96,1]{3,1,4,2,0:T(8,128)S(1)} fusion(f32[2,12,96,96]{3,0,2,1:T(2,128)S(1)} %bitcast.129, f32[1,2,96,192]{2,3,0,1:T(8,128)S(1)} %copy-done.6, f32[1,2,96,192]{2,3,0,1:T(8,128)S(1)} %copy-done.4), kind=kOutput, calls=%fused_computation.12 | convolution fusion | flops 509681664 | bytes 2949120 | tf_op jit(solution)/shard_map/nckxy,cdyl->ndkxl/dot_general | solution.py:30
  52.4 0.0 copy-start
  52.4 2.1 %fusion.5 = f32[2,192,12,192,1]{3,1,2,4,0:T(8,128)S(1)} fusion(f32[2,192,12,96,1]{3,1,4,2,0:T(8,128)S(1)} %fusion.12, f32[1,2,96,192]{2,3,0,1:T(8,128)S(1)} %copy-done.6, f32[1,2,96,192]{2,3,0,1:T(8,128)S(1)} %copy-done.4), kind=kOutput, calls=%fused_computation.5 | convolution fusion | flops 1019289600 | bytes 5603328 | tf_op jit(solution)/shard_map/nckxl,cdxm->ndklm/dot_general | solution.py:30
  54.5 0.0 copy-done
  54.5 2.2 %fusion.1 = f32[2,96,12,192,1]{3,1,2,4,0:T(8,128)S(1)} fusion(f32[2,192,12,192,1]{3,1,2,4,0:T(8,128)S(1)} %fusion.5, f32[12,192,192]{1,2,0:T(8,128)S(1)} %copy-done, f32[1,2,192,96]{2,3,0,1:T(8,128)S(1)} %get-tuple-element.52, f32[1,2,192,96]{2,3,0,1:T(8,128)S(1)} %get-tuple-element.51), kind=kOutput, calls=%fused_computation.2 | convolution fusion | flops 1020174336 | bytes 7372800 | tf_op jit(solution)/shard_map/ncklm,cdmx->ndklx/dot_general | solution.py:30
  56.7 0.0 copy-done.7
  56.7 0.0 copy-done.9
  56.7 1.4 %fusion.8 = f32[1,2,12,96,96]{3,4,2,1,0:T(8,128)S(1)} fusion(f32[2,96,12,192,1]{3,1,2,4,0:T(8,128)S(1)} %fusion.1, f32[1,2,192,96]{2,3,0,1:T(8,128)S(1)} %get-tuple-element.52, f32[1,2,192,96]{2,3,0,1:T(8,128)S(1)} %get-tuple-element.51), kind=kOutput, calls=%fused_computation.8 | convolution fusion | flops 509681664 | bytes 2949120 | tf_op jit(solution)/shard_map/ncklx,cdly->ndkxy/dot_general | solution.py:30
  58.2 0.8 copy.92
  59.0 21.7 %all_to_all.30 = f32[1,2,12,96,96]{4,1,2,0,3:T(2,128)S(1)} all-to-all(f32[1,2,12,96,96]{4,1,2,0,3:T(2,128)S(1)} %copy.92), channel_id=1, replica_groups=mesh['grp'=8,'slab'=16] {'slab'}, dimensions={3} | all-to-all | bytes 1769472 | tf_op jit(solution)/shard_map/all_to_all | solution.py:58
  80.7 0.0 copy-start.8
  80.7 0.0 copy-start.10
  80.7 0.5 copy.93
  81.2 0.4 copy.94
  81.7 0.0 copy-done.8
  81.7 0.0 copy-done.10
  81.7 0.0 copy-start.2
  81.7 0.7 convolution_bitcast_fusion.1
  82.5 0.1 copy.97
  82.6 0.3 squeeze.8
  82.9 0.1 copy.96
  83.1 0.3 squeeze.7
  83.4 0.0 copy-done.2
  83.4 2.1 %fusion.45 = (f32[1,6,9216]{2,0,1:T(1,128)S(1)}, f32[1,6,9216]{2,0,1:T(1,128)S(1)}, f32[1,6,9216]{2,0,1:T(1,128)S(1)}, f32[1,6,9216]{2,0,1:T(1,128)S(1)}) fusion(f32[1,6,9216]{2,0,1:T(1,128)S(1)} %squeeze.7, f32[2,6,9216]{2,0,1:T(2,128)} %get-tuple-element.61, pred[]{:T(512)S(6)} %eq.6, f32[1,6,9216]{2,0,1:T(1,128)S(1)} %squeeze.8, ...), kind=kLoop, calls=%fused_computation.71 | loop fusion | flops 442368 | bytes 2211841 | tf_op jit(solution)/shard_map/mul | solution.py:81
  85.5 0.4 pad_maximum_fusion
  85.9 13.9 %conditional.3 = (f32[2,6,9216]{2,0,1:T(2,128)}) conditional(s32[]{:T(128)} %clamp.4, f32[2,6,9216]{2,0,1:T(2,128)S(1)} %pad_maximum_fusion, f32[2,6,9216]{2,0,1:T(2,128)S(1)} %pad_maximum_fusion, f32[2,6,9216]{2,0,1:T(2,128)S(1)} %pad_maximum_fusion, f32[2,6,9216]{2,0,1:T(2,128)S(1)} %pad_maximum_fusion, ...), branch_computations={%region_7.8_spmd, %region_8.9_spmd, %region_9.10_spmd, %region_10.... | conditional | bytes 1769520 | solution.py:19
  86.0 3.3 %collective-permute-start.10 = (f32[2,6,9216]{2,0,1:T(2,128)S(1)}, f32[2,6,9216]{2,0,1:T(2,128)}, u32[]{:S(2)}, u32[]{:S(2)}) collective-permute-start(f32[2,6,9216]{2,0,1:T(2,128)S(1)} %param.10), channel_id=1, source_target_pairs={{0,64},{16,80},{32,96},{48,112},{64,0},{80,16},{96,32},{112,48},{1... | collective-permute-start | bytes 1327112 | tf_op jit(solution)/shard_map/cond/branch_3_fun/ppermute | solution.py:16
  89.3 10.5 %collective-permute-done.10 = f32[2,6,9216]{2,0,1:T(2,128)} collective-permute-done((f32[2,6,9216]{2,0,1:T(2,128)S(1)}, f32[2,6,9216]{2,0,1:T(2,128)}, u32[]{:S(2)}, u32[]{:S(2)}) %collective-permute-start.10) | collective-permute-done | bytes 442400 | tf_op jit(solution)/shard_map/cond/branch_3_fun/ppermute | solution.py:16
  99.8 2.3 %fusion.18 = f32[2,6,9216]{2,0,1:T(2,128)} fusion(f32[2,6,9216]{2,0,1:T(2,128)} %get-tuple-element.62, f32[1,6,9216]{2,0,1:T(1,128)S(1)} %get-tuple-element.48, f32[1,6,9216]{2,0,1:T(1,128)S(1)} %get-tuple-element.47, f32[2]{0:T(128)S(1)} %get-tuple-element.55), kind=kLoop, calls=%fused_computation.20 | loop fusion | flops 331776 | bytes 1327112 | tf_op jit(solution)/shard_map/mul | solution.py:91
  (3 shorter events, 0.1 us)
Async XLA Ops:
  3.4 19.0 %copy-start.1 = (f32[2,6,9216]{2,0,1:T(2,128)}, f32[2,6,9216]{2,0,1:T(2,128)S(1)}, u32[]{:S(2)}) copy-start(f32[2,6,9216]{2,0,1:T(2,128)S(1)} %broadcast_multiply_fusion) | copy-start | bytes 1327108
  3.4 14.3 %collective-permute-start.3 = (f32[2,6,9216]{2,0,1:T(2,128)S(1)}, f32[2,6,9216]{2,0,1:T(2,128)}, u32[]{:S(2)}, u32[]{:S(2)}) collective-permute-start(f32[2,6,9216]{2,0,1:T(2,128)S(1)} %param.3), channel_id=1, source_target_pairs={{0,64},{16,80},{32,96},{48,112},{64,0},{80,16},{96,32},{112,48},{1... | collective-permute-start | bytes 1327112 | tf_op jit(solution)/shard_map/cond/branch_3_fun/ppermute | solution.py:16
  20.9 0.7 copy-start.3
  21.0 0.8 copy-start.5
  24.3 26.4 %all-to-all-start = ((f32[1,2,192,6,96]{4,1,3,0,2:T(2,128)}), f32[1,2,192,6,96]{4,1,3,0,2:T(2,128)S(1)}, u32[]{:S(2)}, u32[]{:S(2)}) async-start(f32[1,2,192,6,96]{4,1,3,0,2:T(2,128)} %copy.85), calls=%async_computation | async-start | bytes 2359296 | tf_op jit(solution)/shard_map/all_to_all | solution.py:59
  35.8 15.4 %copy-start.4 = (f32[1,2,96,192]{2,3,0,1:T(8,128)S(1)}, f32[1,2,96,192]{2,3,0,1:T(8,128)}, u32[]{:S(2)}) copy-start(f32[1,2,96,192]{2,3,0,1:T(8,128)} %copy-done.3) | copy-start | bytes 442372
  35.8 15.4 %copy-start.6 = (f32[1,2,96,192]{2,3,0,1:T(8,128)S(1)}, f32[1,2,96,192]{2,3,0,1:T(8,128)}, u32[]{:S(2)}) copy-start(f32[1,2,96,192]{2,3,0,1:T(8,128)} %copy-done.5) | copy-start | bytes 442372
  36.7 20.0 %copy-start.7 = (f32[1,2,192,96]{2,3,0,1:T(8,128)}, f32[1,2,192,96]{2,3,0,1:T(8,128)S(1)}, u32[]{:S(2)}) copy-start(f32[1,2,192,96]{2,3,0,1:T(8,128)S(1)} %get-tuple-element.51) | copy-start | bytes 442372
  36.7 20.0 %copy-start.9 = (f32[1,2,192,96]{2,3,0,1:T(8,128)}, f32[1,2,192,96]{2,3,0,1:T(8,128)S(1)}, u32[]{:S(2)}) copy-start(f32[1,2,192,96]{2,3,0,1:T(8,128)S(1)} %get-tuple-element.52) | copy-start | bytes 442372
  52.4 2.1 %copy-start = (f32[12,192,192]{1,2,0:T(8,128)S(1)}, f32[12,192,192]{1,2,0:T(8,128)}, u32[]{:S(2)}) copy-start(f32[12,192,192]{1,2,0:T(8,128)} %copy.89) | copy-start | bytes 5308420
  80.7 1.0 copy-start.8
  80.7 1.0 copy-start.10
  81.7 1.7 %copy-start.2 = (f32[2,6,9216]{2,0,1:T(2,128)S(1)}, f32[2,6,9216]{2,0,1:T(2,128)}, u32[]{:S(2)}) copy-start(f32[2,6,9216]{2,0,1:T(2,128)} %copy-done.1) | copy-start | bytes 1327108
  86.0 13.9 %collective-permute-start.10 = (f32[2,6,9216]{2,0,1:T(2,128)S(1)}, f32[2,6,9216]{2,0,1:T(2,128)}, u32[]{:S(2)}, u32[]{:S(2)}) collective-permute-start(f32[2,6,9216]{2,0,1:T(2,128)S(1)} %param.10), channel_id=1, source_target_pairs={{0,64},{16,80},{32,96},{48,112},{64,0},{80,16},{96,32},{112,48},{1... | collective-permute-start | bytes 1327112 | tf_op jit(solution)/shard_map/cond/branch_3_fun/ppermute | solution.py:16

commit v2 on v1

v2 whole, which is shorter than its diff:
```python
import functools
import math

import jax
import jax.numpy as jnp
import numpy as np
from jax import lax
from jax.experimental import pallas as pl
from jax.experimental.pallas import tpu as pltpu
from jax.sharding import PartitionSpec as P

G = 96
N = 192
SLABS = 16
XS = 6
KP = 6
ROWS = 112

Y_ORDER = np.array([4 * (i % 24) + i // 24 for i in range(G)])
X_ORDER = np.array([6 * (i % SLABS) + i // SLABS for i in range(G)])


def split(table):
    table = jnp.asarray(table, jnp.float32)
    high = table.astype(jnp.bfloat16)
    low = (table - high.astype(jnp.float32)).astype(jnp.bfloat16)
    return high, low


def np_split(table):
    bf16 = jnp.bfloat16
    high = table.astype(np.float32).astype(bf16)
    low = (table - high.astype(np.float64)).astype(np.float32).astype(bf16)
    return np.stack([high, low])


def waves(freq, cell):
    angle = (np.outer(freq, cell) % N) * (2.0 * math.pi / N)
    return np.cos(angle), np.sin(angle)


@functools.cache
def tables():
    pair_major = np.array([[12 * d + 2 * kp for d in range(SLABS)] for kp in range(KP)]).reshape(-1)
    tz = np.zeros((384, 256))
    tv = np.zeros((256, 384))
    wy = np.zeros((2, 256, 512))
    wi = np.zeros((2, 512, 256))
    for kz2 in range(2):
        cos, sin = waves(pair_major + kz2, np.arange(G))
        re, im = 192 * kz2, 192 * kz2 + 96
        tz[re : re + 96, 0:96], tz[re : re + 96, 128:224] = cos, sin
        tz[im : im + 96, 0:96], tz[im : im + 96, 128:224] = -sin, cos
        tv[0:96, re : re + 96], tv[0:96, im : im + 96] = cos.T / N, -sin.T / N
        tv[128:224, re : re + 96], tv[128:224, im : im + 96] = sin.T / N, cos.T / N
        cos, sin = waves(Y_ORDER, np.arange(N))
        re, im = 64 * kz2, 64 * kz2 + 96
        wy[kz2, re : re + 96, 0:192], wy[kz2, re : re + 96, 256:448] = cos, -sin
        wy[kz2, im : im + 96, 0:192], wy[kz2, im : im + 96, 256:448] = sin, cos
        wi[kz2, 0:192, re : re + 96], wi[kz2, 0:192, im : im + 96] = cos.T / N, sin.T / N
        wi[kz2, 256:448, re : re + 96], wi[kz2, 256:448, im : im + 96] = -sin.T / N, cos.T / N
    cos, sin = waves(np.arange(N), X_ORDER)
    tx = np.block([[cos, sin], [-sin, cos]])
    ti = np.block([[cos.T, -sin.T], [sin.T, cos.T]]) / N
    return [np_split(t) for t in (tz, wy, tx, ti, wi, tv)]


def mm(left, right, form=(1, 0)):
    def one(a, b):
        return lax.dot_general(
            a, b, (((form[0],), (form[1],)), ((), ())), preferred_element_type=jnp.float32
        )

    return one(left[0], right[0]) + (one(left[0], right[1]) + one(left[1], right[0]))


def plane(ref, x, orbital):
    base = 144 * x + orbital
    tiles = [ref[pl.ds(base + 2 * tile, 24, stride=6), :] for tile in range(3)]
    return jnp.concatenate(tiles, axis=1)


def lines(dense):
    return jnp.concatenate([dense[:, 96 * q : 96 * q + 96] for q in range(4)], axis=0)


def dense_of(rows):
    return jnp.concatenate([rows[24 * q : 24 * q + 24] for q in range(4)], axis=1)


def spread_kernel(upper_ref, own_ref, their_ref, tz_ref, out_ref):
    upper = upper_ref[0] == 1
    table = (tz_ref[0], tz_ref[1])
    pad = jnp.zeros((G, 32), jnp.float32)
    for x in range(XS):
        theirs = [plane(their_ref, x, o) for o in range(2)]
        first = jnp.where(upper, theirs[1], theirs[0])
        second = jnp.where(upper, theirs[0], theirs[1])
        one = lines(plane(own_ref, x, 0) * first)
        two = lines(plane(own_ref, x, 1) * second)
        density = jnp.concatenate([one, pad, two, pad], axis=1)
        lined = mm(table, split(density), (1, 1))
        wide = jnp.concatenate([lined[96 * j : 96 * j + 96] for j in range(4)], axis=1)
        for kp in range(KP):
            for tile in range(3):
                out_ref[pl.ds(36 * tile + 6 * x + kp, SLABS, stride=ROWS), :] = wide[
                    16 * kp : 16 * kp + 16, 128 * tile : 128 * tile + 128
                ]


def line_kernel(in_ref, hat_ref, wy_ref, tx_ref, ti_ref, wi_ref, out_ref, y_ref, u_ref):
    pieces = []
    for kp in range(KP):
        for x in range(XS):
            pieces.append(
                jnp.concatenate(
                    [
                        in_ref[pl.ds(36 * tile + 6 * x + kp, SLABS, stride=ROWS), :]
                        for tile in range(3)
                    ],
                    axis=1,
                )
            )
    data = split(jnp.concatenate(pieces, axis=0))
    for kz2 in range(2):
        window = [part[:, 128 * kz2 : 128 * kz2 + 256] for part in data]
        result = mm(window, (wy_ref[0, kz2], wy_ref[1, kz2]))
        for kp in range(KP):
            rows = result[96 * kp : 96 * kp + 96]
            y_ref[2 * kp + kz2] = jnp.concatenate([rows[:, :256], rows[:, 256:]], axis=0)

    def one_frequency(kz, carry):
        lined = split(y_ref[kz])
        spectrum = mm((tx_ref[0], tx_ref[1]), lined)
        hat = hat_ref[kz]
        scaled = jnp.concatenate([spectrum[:N] * hat, spectrum[N:] * hat], axis=0)
        u_ref[kz] = mm((ti_ref[0], ti_ref[1]), split(scaled))
        return carry

    lax.fori_loop(0, 2 * KP, one_frequency, 0)
    sides = []
    for kz2 in range(2):
        rows = [
            jnp.concatenate([u_ref[2 * kp + kz2, :G], u_ref[2 * kp + kz2, G:]], axis=1)
            for kp in range(KP)
        ]
        back = jnp.concatenate(rows, axis=0)
        sides.append(mm(split(back), (wi_ref[0, kz2], wi_ref[1, kz2])))
    wide = [sides[0][:, :128], sides[0][:, 128:] + sides[1][:, :128], sides[1][:, 128:]]
    for kp in range(KP):
        for x in range(XS):
            for tile in range(3):
                row = 96 * kp + 16 * x
                out_ref[pl.ds(36 * tile + 6 * x + kp, SLABS, stride=ROWS), :] = wide[tile][
                    row : row + 16
                ]


def term_kernel(upper_ref, weight_ref, in_ref, own_ref, their_ref, tv_ref, kept_ref, sent_ref):
    upper = upper_ref[0] == 1
    table = (tv_ref[0], tv_ref[1])
    for x in range(XS):
        pieces = [
            jnp.concatenate(
                [
                    in_ref[pl.ds(36 * tile + 6 * x + kp, SLABS, stride=ROWS), :]
                    for tile in range(3)
                ],
                axis=1,
            )
            for kp in range(KP)
        ]
        wide = jnp.concatenate(pieces, axis=0)
        stacked = jnp.concatenate([wide[:, 96 * j : 96 * j + 96] for j in range(4)], axis=0)
        fields = mm(table, split(stacked)).T
        one = dense_of(fields[:, :96])
        two = dense_of(fields[:, 128:224])
        theirs = [plane(their_ref, x, o) for o in range(2)]
        first = jnp.where(upper, theirs[1], theirs[0])
        second = jnp.where(upper, theirs[0], theirs[1])
        kept = [one * first, two * second]
        mine_one = one * plane(own_ref, x, 0) * weight_ref[0]
        mine_two = two * plane(own_ref, x, 1) * weight_ref[1]
        sent = [jnp.where(upper, mine_two, mine_one), jnp.where(upper, mine_one, mine_two)]
        for o in range(2):
            for tile in range(3):
                place = pl.ds(144 * x + o + 2 * tile, 24, stride=6)
                kept_ref[place, :] = kept[o][:, 128 * tile : 128 * tile + 128]
                sent_ref[place, :] = sent[o][:, 128 * tile : 128 * tile + 128]
    row = lax.broadcasted_iota(jnp.int32, (8, 128), 0)
    sent_ref[864:872, :] = jnp.where(row % 2 == 1, weight_ref[1], weight_ref[0])


def sum_kernel(upper_ref, kept_ref, come_ref, out_ref):
    upper = upper_ref[0] == 1
    even = jnp.where(upper, come_ref[865:866, :], come_ref[864:865, :])
    odd = jnp.where(upper, come_ref[864:865, :], come_ref[865:866, :])
    row = lax.broadcasted_iota(jnp.int32, (864, 128), 0)
    weight = jnp.where(row % 2 == 0, even, odd)
    out_ref[...] = -(kept_ref[...] * weight + come_ref[0:864, :])


SMEM = pl.BlockSpec(memory_space=pltpu.SMEM)
VMEM = pl.BlockSpec(memory_space=pltpu.VMEM)


def call(kernel, ins, outs, args, scratch=()):
    shapes = [jax.ShapeDtypeStruct(s, jnp.float32) for s in outs]
    return pl.pallas_call(
        kernel,
        out_shape=shapes if len(shapes) > 1 else shapes[0],
        in_specs=ins,
        out_specs=[VMEM] * len(outs) if len(outs) > 1 else VMEM,
        scratch_shapes=scratch,
        compiler_params=pltpu.CompilerParams(vmem_limit_bytes=48 * 1024 * 1024),
    )(*args)


def to_partner(value, pair_bits):
    group_count = lax.axis_size("grp")

    def by_mask(mask):
        pairs = [(source, source ^ mask) for source in range(group_count)]
        return lambda sent: lax.ppermute(sent, "grp", pairs)

    branches = [by_mask(mask) for mask in range(1, group_count)]
    return lax.switch(pair_bits - 1, branches, value)


def to_rows(planes):
    return planes.reshape(2, XS, 72, 128).transpose(1, 2, 0, 3).reshape(864, 128)


def from_rows(rows):
    return rows.reshape(XS, 72, 2, 128).transpose(2, 0, 1, 3).reshape(2, XS, G * G)


def exchange(chunks):
    chunks = chunks.reshape(SLABS, ROWS, 128)
    moved = lax.all_to_all(chunks, "slab", split_axis=0, concat_axis=0, tiled=True)
    return moved.reshape(SLABS * ROWS, 128)


def local(orbitals, occupation, kernel_hat, pair_mask):
    tz, wy, tx, ti, wi, tv = [jnp.asarray(t) for t in tables()]
    pair_bits = pair_mask[0]
    own_group = lax.axis_index("grp")
    upper = (own_group > jnp.bitwise_xor(own_group, pair_bits)).astype(jnp.int32).reshape(1)
    weights = 0.25 * occupation.astype(jnp.float32)
    own = to_rows(orbitals)
    theirs = to_partner(own, pair_bits)
    chunk = (SLABS * ROWS, 128)
    spread = call(spread_kernel, [SMEM, VMEM, VMEM, VMEM], [chunk], (upper, own, theirs, tz))
    hat = kernel_hat.reshape(2 * KP, N, N).transpose(0, 2, 1)
    hat = jnp.pad(hat, ((0, 0), (0, 0), (0, 256 - N)))
    scratch = [pltpu.VMEM((2 * KP, N, 256), jnp.float32)] * 2
    lined = call(
        line_kernel, [VMEM] * 6, [chunk], (exchange(spread), hat, wy, tx, ti, wi), scratch
    )
    back = exchange(lined)
    kept, sent = call(
        term_kernel,
        [SMEM, SMEM, VMEM, VMEM, VMEM, VMEM],
        [(864, 128), (872, 128)],
        (upper, weights, back, own, theirs, tv),
    )
    come = to_partner(sent, pair_bits)
    return from_rows(call(sum_kernel, [SMEM, VMEM, VMEM], [(864, 128)], (upper, kept, come)))


def solution(mesh):
    return jax.shard_map(
        local,
        mesh=mesh,
        in_specs=(P("grp", "slab", None), P("grp"), P("slab", None), P()),
        out_specs=P("grp", "slab", None),
        check_vma=False,
    )
```

time: 101 us -> 95.5 us (0.946); the launches traced: 102 us -> 94.9 us
  Pallas kernels: 0 us -> 22.8 us
  blocking collectives: 21.7 us -> 0 us
  other arithmetic: 11.3 us -> 0.01 us
  waiting for transfers between devices: 34.8 us -> 45.9 us
  matrix products: 8.18 us -> 0 us
    pallas_call x0 -> x4, Pallas kernels: none -> 22.8 us  [call(): pl.pallas_call(kernel, out_shape=shapes if len(shapes) > 1 else shapes[0]...]
    all_to_all x1 -> x0, blocking collectives: 21.7 us -> none  [packed_potential(): lax.all_to_all(line_work(lax.all_to_all(spread, 'slab', split_axis=2, con...]
    all_to_all x1 -> x2, waiting for transfers between devices: 14 us -> 25.1 us  [exchange(): lax.all_to_all(chunks, 'slab', split_axis=0, concat_axis=0, tiled=True)]
    mul x4 -> x1, other arithmetic: 8.5 us -> 0.01 us  [local(): weights = 0.25 * occupation.astype(jnp.float32)]
    dot_general x6 -> x0, matrix products: 8.18 us -> none  [contract(): jnp.einsum(form, left, right, precision=lax.Precision.HIGH, preferred_ele...]
    reshape x0 -> x2, local copies, waits for them, and re-layouts: none -> 4.47 us  [local(): hat = kernel_hat.reshape(2 * KP, N, N).transpose(0, 2, 1)]
    mul x2 -> x0, local copies, waits for them, and re-layouts: 4.47 us -> none  [line_work(): spectra = spectra * kernel_cube[None, None]]
    all_to_all x1 -> x2, starting transfers between devices: 7.04 us -> 10.7 us  [exchange(): lax.all_to_all(chunks, 'slab', split_axis=0, concat_axis=0, tiled=True)]
  transfers between devices with their start and end apart: 3 -> 4, of which waited for: 3 -> 4; matrix products, arithmetic and copies ran while one was open for 5% -> 8% of each run, Pallas kernels for 0% -> 0%
where the time goes in v2:
time: 95.5 us; the launch traced here: 94.9 us
  waiting for transfers between devices  45.9 us (48%)
  Pallas kernels  22.8 us (24%)
  starting transfers between devices  14.6 us (15%)
  local copies, waits for them, and re-layouts  10.8 us (11%)
    all_to_all x2, waiting for transfers between devices, exchange(): lax.all_to_all(chunks, 'slab', split_axis=0, concat_axis=0, tiled=True)  25.1 us
    pallas_call x4, Pallas kernels, call(): pl.pallas_call(kernel, out_shape=shapes if len(shapes) > 1 else shapes[0]...  22.8 us
    ppermute x2, waiting for transfers between devices, by_mask(): return lambda sent: lax.ppermute(sent, 'grp', pairs)  20.8 us
    all_to_all x2, starting transfers between devices, exchange(): lax.all_to_all(chunks, 'slab', split_axis=0, concat_axis=0, tiled=True)  10.7 us
    reshape x2, local copies, waits for them, and re-layouts, local(): hat = kernel_hat.reshape(2 * KP, N, N).transpose(0, 2, 1)  4.47 us
    ppermute x2, starting transfers between devices, by_mask(): return lambda sent: lax.ppermute(sent, 'grp', pairs)  3.93 us
    pad x1, local copies, waits for them, and re-layouts, local(): hat = jnp.pad(hat, ((0, 0), (0, 0), (0, 256 - N)))  3.41 us
    unnamed x14, local copies, waits for them, and re-layouts  2.97 us
  transfers between devices with their start and end apart: 4, of which 4 were waited for; matrix products, arithmetic and copies ran while one was open for 8% of the time, Pallas kernels for 0%

profile of v2, /device:TPU:0, one launch (start us, length us, event | category | flops | bytes accessed | tf_op | source)
XLA Modules:
  0.0 94.9 jit_solution(14733170892639991565)
XLA Ops:
  0.7 12.6 %conditional.2 = (f32[864,128]{1,0:T(8,128)}) conditional(s32[]{:T(128)} %clamp.4, f32[864,128]{1,0:T(8,128)} %bitcast.22, f32[864,128]{1,0:T(8,128)} %bitcast.23, f32[864,128]{1,0:T(8,128)} %bitcast.24, f32[864,128]{1,0:T(8,128)} %bitcast.25, f32[864,128]{1,0:T(8,128)} %bitcast.26, f32[864,128]{1,0:T(8,128)} %bitcast.27, ...), branch_computations={%region_0.0_spmd, %region_1.0_spmd, %region_2.0_spmd, %region_3.0_... | conditional | bytes 1769520 | solution.py:227
  0.7 2.1 %collective-permute-start.1 = (f32[864,128]{1,0:T(8,128)}, f32[864,128]{1,0:T(8,128)}, u32[]{:S(2)}, u32[]{:S(2)}) collective-permute-start(f32[864,128]{1,0:T(8,128)} %param.1), channel_id=1, source_target_pairs={{0,32},{16,48},{32,0},{48,16},{64,96},{80,112},{96,64},{112,80},{1... | collective-permute-start | bytes 1327112 | tf_op jit(solution)/shard_map/cond/branch_1_fun/ppermute | solution.py:224
  2.8 10.5 %collective-permute-done.1 = f32[864,128]{1,0:T(8,128)} collective-permute-done((f32[864,128]{1,0:T(8,128)}, f32[864,128]{1,0:T(8,128)}, u32[]{:S(2)}, u32[]{:S(2)}) %collective-permute-start.1) | collective-permute-done | bytes 442400 | tf_op jit(solution)/shard_map/cond/branch_1_fun/ppermute | solution.py:224
  13.3 0.0 copy-start.2
  13.3 1.0 %copy-done.2 = bf16[2,384,256]{2,1,0:T(8,128)(2,1)S(1)} copy-done((bf16[2,384,256]{2,1,0:T(8,128)(2,1)S(1)}, bf16[2,384,256]{2,1,0:T(8,128)(2,1)}, u32[]{:S(2)}) %copy-start.2) | copy-done | bytes 393240
  14.3 3.4 %shard_map.100 = f32[1792,128]{1,0:T(8,128)} custom-call(s32[1]{0:T(128)} %bitcast.1.upper_ref, f32[864,128]{1,0:T(8,128)} %bitcast.29, f32[864,128]{1,0:T(8,128)} %get-tuple-element.39.their_ref, bf16[2,384,256]{2,1,0:T(8,128)(2,1)S(1)} %copy-done.2), custom_call_target="tpu_custom_call" | custom-call | tf_op jit(solution)/shard_map/pallas_call | solution.py:209
  17.7 7.0 %all-to-all-start = ((f32[16,112,128]{2,1,0:T(8,128)}), f32[16,112,128]{2,1,0:T(8,128)S(1)}, u32[]{:S(2)}, u32[]{:S(2)}) async-start(f32[16,112,128]{2,1,0:T(8,128)} %bitcast.7), calls=%async_computation | async-start | bytes 1835008 | tf_op jit(solution)/shard_map/all_to_all | solution.py:240
  24.7 2.3 %reshape.59 = f32[12,192,192]{2,1,0:T(8,128)S(1)} reshape(f32[12,36864]{1,0:T(8,128)} %param.26) | data formatting | bytes 3538944 | tf_op jit(solution)/shard_map/reshape | solution.py:254
  27.1 2.1 %copy.14 = f32[12,192,192]{1,2,0:T(8,128)} copy(f32[12,192,192]{2,1,0:T(8,128)S(1)} %reshape.59) | data formatting | bytes 3538944 | tf_op jit(solution)/shard_map/reshape | solution.py:254
  29.2 0.0 copy-start
  29.2 0.0 copy-start.1
  29.2 3.4 %pad.4.hat_ref = f32[12,192,256]{2,1,0:T(8,128)} pad(f32[12,192,192]{2,1,0:T(8,128)} %bitcast.21, f32[]{:T(128)} %constant.28.clone.1), padding=0_0x0_0x0_64 | pad | bytes 4128772 | tf_op jit(solution)/shard_map/jit(_pad)/pad | solution.py:255
  32.6 8.7 %all-to-all-done = f32[16,112,128]{2,1,0:T(8,128)S(1)} async-done(((f32[16,112,128]{2,1,0:T(8,128)}), f32[16,112,128]{2,1,0:T(8,128)S(1)}, u32[]{:S(2)}, u32[]{:S(2)}) %all-to-all-start) | async-done | bytes 917536 | tf_op jit(solution)/shard_map/all_to_all | solution.py:240
  41.3 0.0 copy-done
  41.3 0.0 copy-done.1
  41.3 0.0 copy-start.4
  41.3 1.0 %copy-done.4 = bf16[2,384,192]{2,1,0:T(8,128)(2,1)S(1)} copy-done((bf16[2,384,192]{2,1,0:T(8,128)(2,1)S(1)}, bf16[2,384,192]{2,1,0:T(8,128)(2,1)}, u32[]{:S(2)}) %copy-start.4) | copy-done | bytes 294936
  42.3 0.0 copy-start.5
  42.3 1.0 %copy-done.5 = bf16[2,192,384]{2,1,0:T(8,128)(2,1)S(1)} copy-done((bf16[2,192,384]{2,1,0:T(8,128)(2,1)S(1)}, bf16[2,192,384]{2,1,0:T(8,128)(2,1)}, u32[]{:S(2)}) %copy-start.5) | copy-done | bytes 294936
  43.3 0.0 copy-start.6
  43.3 0.0 copy-start.3
  43.3 14.9 %shard_map.101 = f32[1792,128]{1,0:T(8,128)} custom-call(f32[1792,128]{1,0:T(8,128)S(1)} %bitcast.20, f32[12,192,256]{2,1,0:T(8,128)} %pad.4.hat_ref, bf16[2,2,256,512]{3,2,1,0:T(8,128)(2,1)S(1)} %copy-done, bf16[2,384,192]{2,1,0:T(8,128)(2,1)S(1)} %copy-done.4, bf16[2,192,384]{2,1,0:T(8,128)(2,1)S(1)} %copy-done.5, bf16[2,2,512,256]{3,2,1,0:T(8,128)(2,1)S(1)} %copy-done.1), custom_call_target="tpu_custom_call" | custom-call | tf_op jit(solution)/shard_map/pallas_call | solution.py:209
  58.2 3.6 %all-to-all-start.1 = ((f32[16,112,128]{2,1,0:T(8,128)}), f32[16,112,128]{2,1,0:T(8,128)S(1)}, u32[]{:S(2)}, u32[]{:S(2)}) async-start(f32[16,112,128]{2,1,0:T(8,128)} %bitcast.10), calls=%async_computation.1 | async-start | bytes 1835008 | tf_op jit(solution)/shard_map/all_to_all | solution.py:240
  61.8 0.0 copy-done.6
  61.9 16.5 %all-to-all-done.1 = f32[16,112,128]{2,1,0:T(8,128)S(1)} async-done(((f32[16,112,128]{2,1,0:T(8,128)}), f32[16,112,128]{2,1,0:T(8,128)S(1)}, u32[]{:S(2)}, u32[]{:S(2)}) %all-to-all-start.1) | async-done | bytes 917536 | tf_op jit(solution)/shard_map/all_to_all | solution.py:240
  78.4 0.0 copy-done.3
  78.4 2.6 %shard_map.102 = (f32[864,128]{1,0:T(8,128)S(1)}, f32[872,128]{1,0:T(8,128)S(1)}) custom-call(s32[1]{0:T(128)} %bitcast.1.upper_ref, f32[2]{0:T(128)S(1)} %convert_multiply_fusion.weight_ref, f32[1792,128]{1,0:T(8,128)S(1)} %bitcast.19, f32[864,128]{1,0:T(8,128)} %bitcast.30, f32[864,128]{1,0:T(8,128)} %get-tuple-element.39.their_ref, ...), custom_call_target="tpu_custom_call" | custom-call | tf_op jit(solution)/shard_map/pallas_call | solution.py:209
  80.9 12.1 %conditional.3 = (f32[872,128]{1,0:T(8,128)}) conditional(s32[]{:T(128)} %clamp.4, f32[872,128]{1,0:T(8,128)S(1)} %get-tuple-element.38, f32[872,128]{1,0:T(8,128)S(1)} %get-tuple-element.38, f32[872,128]{1,0:T(8,128)S(1)} %get-tuple-element.38, f32[872,128]{1,0:T(8,128)S(1)} %get-tuple-element.38, ...), branch_computations={%region_7.8_spmd, %region_8.9_spmd, %region_9.10_spmd, %region_10.... | conditional | bytes 1785904 | solution.py:227
  80.9 1.8 %collective-permute-start.8 = (f32[872,128]{1,0:T(8,128)S(1)}, f32[872,128]{1,0:T(8,128)}, u32[]{:S(2)}, u32[]{:S(2)}) collective-permute-start(f32[872,128]{1,0:T(8,128)S(1)} %param.8), channel_id=1, source_target_pairs={{0,32},{16,48},{32,0},{48,16},{64,96},{80,112},{96,64},{112,80},{1... | collective-permute-start | bytes 1339400 | tf_op jit(solution)/shard_map/cond/branch_1_fun/ppermute | solution.py:224
  82.8 10.3 %collective-permute-done.8 = f32[872,128]{1,0:T(8,128)} collective-permute-done((f32[872,128]{1,0:T(8,128)S(1)}, f32[872,128]{1,0:T(8,128)}, u32[]{:S(2)}, u32[]{:S(2)}) %collective-permute-start.8) | collective-permute-done | bytes 446496 | tf_op jit(solution)/shard_map/cond/branch_1_fun/ppermute | solution.py:224
  93.0 1.9 %shard_map.103 = f32[864,128]{1,0:T(8,128)} custom-call(s32[1]{0:T(128)} %bitcast.1.upper_ref, f32[864,128]{1,0:T(8,128)S(1)} %get-tuple-element.37.kept_ref, f32[872,128]{1,0:T(8,128)} %get-tuple-element.40.come_ref), custom_call_target="tpu_custom_call" | custom-call | tf_op jit(solution)/shard_map/pallas_call | solution.py:209
  (1 shorter events, 0.0 us)
Async XLA Ops:
  0.7 12.6 %collective-permute-start.1 = (f32[864,128]{1,0:T(8,128)}, f32[864,128]{1,0:T(8,128)}, u32[]{:S(2)}, u32[]{:S(2)}) collective-permute-start(f32[864,128]{1,0:T(8,128)} %param.1), channel_id=1, source_target_pairs={{0,32},{16,48},{32,0},{48,16},{64,96},{80,112},{96,64},{112,80},{1... | collective-permute-start | bytes 1327112 | tf_op jit(solution)/shard_map/cond/branch_1_fun/ppermute | solution.py:224
  13.3 1.0 %copy-start.2 = (bf16[2,384,256]{2,1,0:T(8,128)(2,1)S(1)}, bf16[2,384,256]{2,1,0:T(8,128)(2,1)}, u32[]{:S(2)}) copy-start(bf16[2,384,256]{2,1,0:T(8,128)(2,1)} %constant.29.clone.tz_ref) | copy-start | bytes 1179652
  17.7 23.6 %all-to-all-start = ((f32[16,112,128]{2,1,0:T(8,128)}), f32[16,112,128]{2,1,0:T(8,128)S(1)}, u32[]{:S(2)}, u32[]{:S(2)}) async-start(f32[16,112,128]{2,1,0:T(8,128)} %bitcast.7), calls=%async_computation | async-start | bytes 1835008 | tf_op jit(solution)/shard_map/all_to_all | solution.py:240
  29.2 12.1 %copy-start = (bf16[2,2,256,512]{3,2,1,0:T(8,128)(2,1)S(1)}, bf16[2,2,256,512]{3,2,1,0:T(8,128)(2,1)}, u32[]{:S(2)}) copy-start(bf16[2,2,256,512]{3,2,1,0:T(8,128)(2,1)} %constant.30.clone.wy_ref) | copy-start | bytes 3145732
  29.2 12.1 %copy-start.1 = (bf16[2,2,512,256]{3,2,1,0:T(8,128)(2,1)S(1)}, bf16[2,2,512,256]{3,2,1,0:T(8,128)(2,1)}, u32[]{:S(2)}) copy-start(bf16[2,2,512,256]{3,2,1,0:T(8,128)(2,1)} %constant.33.clone.wi_ref) | copy-start | bytes 3145732
  41.3 1.0 %copy-start.4 = (bf16[2,384,192]{2,1,0:T(8,128)(2,1)S(1)}, bf16[2,384,192]{2,1,0:T(8,128)(2,1)}, u32[]{:S(2)}) copy-start(bf16[2,384,192]{2,1,0:T(8,128)(2,1)} %constant.31.clone.tx_ref) | copy-start | bytes 884740
  42.3 1.0 %copy-start.5 = (bf16[2,192,384]{2,1,0:T(8,128)(2,1)S(1)}, bf16[2,192,384]{2,1,0:T(8,128)(2,1)}, u32[]{:S(2)}) copy-start(bf16[2,192,384]{2,1,0:T(8,128)(2,1)} %constant.32.clone.ti_ref) | copy-start | bytes 884740
  43.3 18.6 %copy-start.6 = (s32[2]{0:T(128)S(1)}, s32[2]{0:T(128)}, u32[]{:S(2)}) copy-start(s32[2]{0:T(128)} %param.25) | copy-start | bytes 28
  43.3 35.1 %copy-start.3 = (bf16[2,256,384]{2,1,0:T(8,128)(2,1)S(1)}, bf16[2,256,384]{2,1,0:T(8,128)(2,1)}, u32[]{:S(2)}) copy-start(bf16[2,256,384]{2,1,0:T(8,128)(2,1)} %constant.34.clone.tv_ref) | copy-start | bytes 1179652
  58.2 20.2 %all-to-all-start.1 = ((f32[16,112,128]{2,1,0:T(8,128)}), f32[16,112,128]{2,1,0:T(8,128)S(1)}, u32[]{:S(2)}, u32[]{:S(2)}) async-start(f32[16,112,128]{2,1,0:T(8,128)} %bitcast.10), calls=%async_computation.1 | async-start | bytes 1835008 | tf_op jit(solution)/shard_map/all_to_all | solution.py:240
  80.9 12.1 %collective-permute-start.8 = (f32[872,128]{1,0:T(8,128)S(1)}, f32[872,128]{1,0:T(8,128)}, u32[]{:S(2)}, u32[]{:S(2)}) collective-permute-start(f32[872,128]{1,0:T(8,128)S(1)} %param.8), channel_id=1, source_target_pairs={{0,32},{16,48},{32,0},{48,16},{64,96},{80,112},{96,64},{112,80},{1... | collective-permute-start | bytes 1339400 | tf_op jit(solution)/shard_map/cond/branch_1_fun/ppermute | solution.py:224
